TPU v7x, 128 devices: a whole 4x4x4 slice. The times are simulated.
128 devices in a mesh: band: 8 (over y, x_lo), chan: 16 (over x_hi, z, core).
Axes of the slice: x: 4 (x_hi: 2, x_lo: 2; x = x_hi * 2 + x_lo), y: 4, z: 4, core: 2. Of those that a mesh axis runs over, the one named last changes fastest.
Arguments:
- coeffs: bfloat16 [2, 8, 1024, 8192], P(None, None, 'chan', 'band'), may hold values from -1100 to 1100, as said below
Outputs:
- coherence: float32 [1024, 1024], P('chan', 'band')
Inputs may be any that keep to these rules, and one draw needn't show every extreme that they name: `coeffs`: finite real and imaginary parts.
All inputs are finite; a program needn't handle non-finite values.
Results may differ from a plain program's by a relative error of at most 0.0003.
Values may be sent and summed in bfloat16 or wider, within the bound.
A program may use at most 192 MiB of HBM per device.

v0:
```python
import jax
import jax.numpy as jnp
from jax import lax
from jax.sharding import PartitionSpec as P

K = 8
W = 16


epsilon = 1e-06


def in_blocks(shard, dim, length):
    dims = shard.shape
    tiles = shard.reshape(*dims[:dim], length, dims[dim] // length, *dims[dim + 1 :])
    return jnp.moveaxis(tiles, dim, 0)


def sent_and_summed(shard, axis, dim):
    length = lax.axis_size(axis)
    tiles = lax.all_to_all(in_blocks(shard, dim, length), axis, 0, 0, tiled=True)
    return jnp.sum(tiles, axis=0)


def body(coeffs):
    num_bands = coeffs.shape[3] // W
    own_width = coeffs.shape[2]
    cycle_size = lax.axis_size("chan")
    own_index = lax.axis_index("chan")
    full_width = own_width * cycle_size
    group_count = lax.axis_size("band")
    scale = jnp.float32(W * K / (num_bands * group_count))
    local_rows = coeffs.reshape(2, K, own_width, num_bands, W)
    paired = jnp.stack((local_rows[1], -local_rows[0]), axis=0)
    left_side = jnp.concatenate((local_rows, paired), axis=2)
    wide_rows = local_rows.astype(jnp.float32)
    own_power = jnp.sum(wide_rows * wide_rows, axis=(0, 1, 4)).T + epsilon
    piece = lax.all_gather(coeffs, "chan", axis=2, tiled=True)
    count = piece.shape[2]
    right_side = piece.reshape(2, K, count, num_bands, W)
    product = jnp.einsum(
        "pkinw,pkjnw->nij", left_side, right_side, preferred_element_type=jnp.float32
    )
    real_part = product[:, :own_width, :]
    imag_part = product[:, own_width:, :]
    wide_piece = right_side.astype(jnp.float32)
    piece_power = jnp.sum(wide_piece * wide_piece, axis=(0, 1, 4)).T + epsilon
    coh_band = (real_part * real_part + imag_part * imag_part) / (
        own_power[:, :, None] * piece_power[:, None, :]
    )
    partial_value = jnp.sum(coh_band, axis=0)
    row_global = lax.broadcasted_iota(jnp.int32, (own_width, full_width), 0) + own_index * own_width
    col_global = lax.broadcasted_iota(jnp.int32, (own_width, full_width), 1)
    partial_value = jnp.where(row_global == col_global, jnp.float32(0.0), partial_value)
    result = sent_and_summed(partial_value, "band", 1)
    return result * scale


def solution(mesh):
    return jax.shard_map(
        body,
        mesh=mesh,
        in_specs=(P(None, None, "chan", "band"),),
        out_specs=P("chan", "band"),
        check_vma=False,
    )
```

profile of v0, /device:TPU:9, one launch (start us, length us, event | category | flops | bytes accessed | tf_op | source)
XLA Modules:
  0.0 324.8 jit_solution(6133088543758207707)
XLA Ops:
  6.5 0.0 copy-start
  6.5 0.0 all-gather.2.cloned.1.call-start
  6.5 4.2 %copy.37 = bf16[2,8,64,1024]{3,1,0,2:T(8,128)(2,1)} copy(bf16[2,8,64,1024]{3,2,1,0:T(8,128)(2,1)} %param.1) | data formatting | bytes 4194304 | tf_op args[0]
  10.7 0.0 all-gather.2.cloned.1.call-update
  10.8 0.0 copy-done
  10.8 3.2 copy.31
  14.0 0.4 multiply_reduce_fusion.1
  14.4 0.2 copy.40
  14.6 0.1 bitcast_reduce_fusion.1
  14.7 4.0 %fusion.14 = (bf16[1,8,64,1024]{2,3,1,0:T(8,128)(2,1)S(1)}, bf16[1,8,64,1024]{2,3,1,0:T(8,128)(2,1)}) fusion(bf16[2,8,64,1024]{2,3,1,0:T(8,128)(2,1)} %copy.31), kind=kLoop, calls=%fused_computation.25 | loop fusion | flops 524288 | bytes 4194304 | tf_op jit(solution)/shard_map/slice | solution.py:34
  18.7 180.6 %all-gather.2.cloned.1.call-done = bf16[2,8,1024,1024]{3,1,0,2:T(8,128)(2,1)} async-done(((bf16[2,8,64,1024]{3,1,0,2:T(8,128)(2,1)}), bf16[2,8,1024,1024]{3,1,0,2:T(8,128)(2,1)}) %all-gather.2.cloned.1.call-update) | async-done | bytes 33554448 | tf_op jit(solution)/shard_map/all_gather | solution.py:38
  199.3 18.3 %multiply_reduce_fusion = f32[1024,1024]{1,0:T(8,128)} fusion(bf16[2,8,1024,1024]{3,1,0,2:T(8,128)(2,1)} %all-gather.2.cloned.1.call-done), kind=kLoop, calls=%fused_computation | loop fusion | flops 49283072 | bytes 37748736 | tf_op jit(solution)/shard_map/reduce_sum | solution.py:47
  217.6 5.3 %copy.41 = f32[1024,1024]{0,1:T(8,128)} copy(f32[1024,1024]{1,0:T(8,128)} %multiply_reduce_fusion) | data formatting | bytes 8388608 | tf_op jit(solution)/shard_map/reduce_sum | solution.py:47
  222.9 3.1 bitcast_reduce_fusion
  226.0 45.1 %copy.38 = bf16[2,8,1024,1024]{2,3,1,0:T(8,128)(2,1)} copy(bf16[2,8,1024,1024]{3,1,0,2:T(8,128)(2,1)} %all-gather.2.cloned.1.call-done) | data formatting | bytes 67108864 | tf_op jit(solution)/shard_map/all_gather | solution.py:38
  271.2 25.2 %fusion.5 = f32[64,128,1024]{2,1,0:T(8,128)} fusion(bf16[2,8,1024,64,16]{2,4,3,1,0:T(8,128)(2,1)} %bitcast.24, bf16[1,8,64,64,16]{2,4,0,3,1:T(8,128)(2,1)} %bitcast.27, bf16[1,8,64,64,16]{2,4,0,3,1:T(8,128)(2,1)S(1)} %bitcast.26, bf16[2,8,64,64,16]{2,4,3,1,0:T(8,128)(2,1)} %bitcast.25), kind=kOutput, calls=%fused_computation.8 | convolution fusion | flops 4307550208 | bytes 71303168 | tf_op jit(solution)/shard_map/pkinw,pkjnw->nij/dot_general | solution.py:41
  296.4 11.9 %fusion.4 = f32[64,1024]{1,0:T(8,128)S(1)} fusion(f32[64,128,1024]{2,1,0:T(8,128)} %fusion.5, f32[64,1024]{1,0:T(8,128)S(1)} %add_bitcast_fusion, f32[64,64]{1,0:T(8,128)S(1)} %add_bitcast_fusion.1), kind=kLoop, calls=%fused_computation.7 | loop fusion | flops 25100288 | bytes 34095104 | tf_op jit(solution)/shard_map/reduce_sum | solution.py:51
  308.3 0.1 bitcast_select_fusion
  308.5 0.1 copy.42
  308.5 8.7 %all_to_all.5 = f32[8,64,128]{2,1,0:T(8,128)S(1)} all-to-all(f32[8,64,128]{2,1,0:T(8,128)S(1)} %copy.42), channel_id=1, replica_groups=mesh['band'=8,'chan'=16] {'band'}, dimensions={0} | all-to-all | bytes 524288 | tf_op jit(solution)/shard_map/all_to_all | solution.py:21
  317.3 0.6 broadcast_multiply_fusion
  (6 shorter events, 0.1 us)
Async XLA Ops:
  6.5 4.2 %copy-start = (bf16[2,8,64,1024]{3,2,1,0:T(8,128)(2,1)S(1)}, bf16[2,8,64,1024]{3,2,1,0:T(8,128)(2,1)}, u32[]{:S(2)}) copy-start(bf16[2,8,64,1024]{3,2,1,0:T(8,128)(2,1)} %param.1) | copy-start | bytes 6291460
  6.5 192.7 %all-gather.2.cloned.1.call-start = ((), (), s32[]{:S(2)}) async-start(), calls=%async_computation.1 | async-start | bytes 35651584 | tf_op jit(solution)/shard_map/all_gather | solution.py:38
Sparse Core Ops, SparseCore 0:
  10.9 188.3 all-gather.1
where the time goes:
time: 329 us; the launch traced here: 325 us
  waiting for transfers between devices  181 us (55%)
  local copies, waits for them, and re-layouts  58.1 us (18%)
  other arithmetic  38.6 us (12%)
  matrix products  25.2 us (8%)
  between operations  13.5 us (4%)
  blocking collectives  8.74 us (3%)
    all_gather x1, waiting for transfers between devices, body(): piece = lax.all_gather(coeffs, 'chan', axis=2, tiled=True)  181 us
    all_gather x1, local copies, waits for them, and re-layouts, body(): piece = lax.all_gather(coeffs, 'chan', axis=2, tiled=True)  45.1 us
    dot_general x1, matrix products, body(): jnp.einsum('pkinw,pkjnw->nij', left_side, right_side, preferred_element_t...  25.2 us
    reduce_sum x2, other arithmetic, body(): piece_power = jnp.sum(wide_piece * wide_piece, axis=(0, 1, 4)).T + epsilon  21.4 us
    reduce_sum x1, other arithmetic, body(): partial_value = jnp.sum(coh_band, axis=0)  11.9 us
    all_to_all x1, blocking collectives, sent_and_summed(): lax.all_to_all(in_blocks(shard, dim, length), axis, 0, 0, tiled=True)  8.74 us
    unnamed x5, local copies, waits for them, and re-layouts  7.43 us
  transfers between devices with their start and end apart: 1, of which 1 were waited for; matrix products, arithmetic and copies ran while one was open for 2% of the time, Pallas kernels for 0%

commit v1 on v0

v1 whole, which is shorter than its diff:
```python
import functools

import jax
import jax.numpy as jnp
from jax import lax
from jax.experimental import pallas as pl
from jax.experimental.pallas import tpu as pltpu
from jax.sharding import PartitionSpec as P

K = 8
W = 16
EPS = 1e-06
MESH = pl.DeviceIdType.MESH
TILES = 36
F32 = jnp.float32
BF16 = jnp.bfloat16


def nt_dot(a, b):
    return lax.dot_general(a, b, (((1,), (1,)), ((), ())), preferred_element_type=F32)


def relayout(src, dst):
    group = lax.broadcasted_iota(jnp.int32, (16, 128), 1) // 16
    bits = [(group // (1 << s)) % 2 == 1 for s in range(3)]
    for part in range(2):
        for r in range(4):
            rows = pl.ds(r * 16, 16)
            vals = []
            for k in range(8):
                v = src[part, k, rows, :].astype(F32)
                vals.append(v if k == 0 else pltpu.roll(v, 16 * k, 1))
            for s in range(3):
                vals = [jnp.where(bits[s], vals[(m + (1 << s)) % 8], vals[m]) for m in range(8)]
            for w in range(8):
                dst[w, rows, part * 128 : (part + 1) * 128] = vals[(8 - w) % 8].astype(BF16)


def split_square(x):
    wide = x.astype(F32)
    square = wide * wide
    high = square.astype(BF16)
    low = (square - high.astype(F32)).astype(BF16)
    return high, low


def kernel(
    scale, cx, out, xin, sbuf, rbuf, lhs, rowi, coli, tacc, yrecv, fsend, frecv, bpad, bt, drecv,
    in_s, p1s, p1r, fws, fwr, ys, yr, fs, fr, ds, dr,
):
    b = lax.axis_index("band")
    ch = lax.axis_index("chan")
    y, xlo = b // 2, b % 2
    g, c = ch // 2, ch % 2
    xhi, z = g // 4, g % 4
    x = xhi * 2 + xlo
    pc = 1 - c

    def member(k):
        return lax.rem(xhi + k // 4, 2) * 4 + lax.rem(z + k, 4)

    def target(k):
        return lax.rem(xhi + k // 4, 2) * 4 + lax.rem(z + 8 - k, 4)

    def dev(band, grp, core):
        return (band, grp * 2 + core)

    barrier = pltpu.get_barrier_semaphore()
    for k in range(1, 8):
        pl.semaphore_signal(barrier, inc=1, device_id=dev(b, target(k), c), device_id_type=MESH)
    pl.semaphore_signal(barrier, inc=1, device_id=dev(b, g, pc), device_id_type=MESH)
    for r in range(1, 4):
        pl.semaphore_signal(
            barrier, inc=1, device_id=dev(lax.rem(y + r, 4) * 2 + xlo, g, c), device_id_type=MESH
        )
    for d in (1, 3):
        xo = lax.rem(x + d, 4)
        pl.semaphore_signal(
            barrier,
            inc=1,
            device_id=dev(y * 2 + xo % 2, (xo // 2) * 4 + z, c),
            device_id_type=MESH,
        )

    def load(k):
        return pltpu.make_async_copy(
            cx.at[:, :, :, pl.ds(pl.multiple_of(target(k) * 128, 128), 128)], xin.at[k], in_s.at[k]
        )

    for k in range(1, 8):
        load(k).start()
    load(0).start()

    def p1(k):
        return pltpu.make_async_remote_copy(
            src_ref=sbuf.at[k],
            dst_ref=rbuf.at[k, c],
            send_sem=p1s.at[k],
            recv_sem=p1r.at[k],
            device_id=dev(b, target(k), c),
            device_id_type=MESH,
        )

    def fwd(k):
        return pltpu.make_async_remote_copy(
            src_ref=rbuf.at[k, c],
            dst_ref=rbuf.at[k, c],
            send_sem=fws.at[k],
            recv_sem=fwr.at[k],
            device_id=dev(b, g, pc),
            device_id_type=MESH,
        )

    def send_loop(k, carry):
        load(k).wait()
        relayout(xin.at[k], sbuf.at[k])

        @pl.when(k == 1)
        def _():
            pl.semaphore_wait(barrier, 13)

        p1(k).start()
        return carry

    lax.fori_loop(1, 8, send_loop, 0)
    load(0).wait()
    relayout(xin.at[0], rbuf.at[0, c])
    fwd(0).start()

    ones_row = jnp.ones((8, 256), BF16)
    ones_col = jnp.ones((128, 256), BF16)

    def ysend(t):
        yt = lax.rem(t, 4)
        return pltpu.make_async_remote_copy(
            src_ref=tacc.at[t],
            dst_ref=yrecv.at[t // 4, lax.rem(y + 3 - yt + 4, 4)],
            send_sem=ys.at[t],
            recv_sem=yr.at[t // 4, lax.rem(y + 3 - yt + 4, 4)],
            device_id=dev(yt * 2 + xlo, g, c),
            device_id_type=MESH,
        )

    def tile(i, j):
        t = i * (i + 1) // 2 + j
        acc = jnp.zeros((64, 128), F32)
        for w in range(8):
            right = rbuf[j, :, w].reshape(128, 256)
            prod = nt_dot(lhs[w], right)
            re, im = prod[:64], prod[64:]
            acc = acc + (re * re + im * im) * (coli[w] * rowi[j, w, 0:1, :])
        tacc[t] = acc

        @pl.when(lax.rem(t, 4) != y)
        def _():
            ysend(t).start()

    def step(i, carry):
        @pl.when(i > 0)
        def _():
            p1(i).wait_recv()
            fwd(i).start()

        for w in range(8):
            v = rbuf[i, c, w]
            lhs[w, 0:64, :] = v
            lhs[w, 64:128, 0:128] = v[:, 128:]
            lhs[w, 64:128, 128:256] = -v[:, :128]
            high, low = split_square(v)
            coli[w] = 1.0 / (nt_dot(high, ones_col) + nt_dot(low, ones_col) + EPS)

        def inner(j, carry2):
            tile(i, j)
            return carry2

        lax.fori_loop(0, i, inner, 0)
        fwd(i).wait_recv()
        for w in range(8):
            high, low = split_square(rbuf[i, :, w].reshape(128, 256))
            rowi[i, w] = 1.0 / (nt_dot(ones_row, high) + nt_dot(ones_row, low) + EPS)
        tile(i, i)
        return carry

    lax.fori_loop(0, 8, step, 0)

    slot = x * 4 + z

    def pair_of(t):
        i = 0
        for m in range(1, 8):
            i = i + jnp.where(t >= m * (m + 1) // 2, 1, 0)
        return i, t - i * (i + 1) // 2

    def fsend_copy(q, side, band, grp):
        return pltpu.make_async_remote_copy(
            src_ref=fsend.at[q],
            dst_ref=frecv.at[slot],
            send_sem=fs.at[q, side],
            recv_sem=fr.at[slot],
            device_id=dev(band, grp, c),
            device_id_type=MESH,
        )

    def is_self(band, grp):
        return jnp.where(band == b, 1, 0) * jnp.where(grp == g, 1, 0)

    def final_loop(q, carry):
        t = q * 4 + y
        i, j = pair_of(t)
        s, u = member(i), member(j)
        total = tacc[t]
        for r in range(3):
            pltpu.make_async_remote_copy(
                src_ref=tacc.at[t],
                dst_ref=yrecv.at[q, r],
                send_sem=ys.at[t],
                recv_sem=yr.at[q, r],
                device_id=dev(b, g, c),
                device_id_type=MESH,
            ).wait_recv()
            total = total + yrecv[q, r]
        fsend[q] = total

        @pl.when(is_self(u, s) == 1)
        def _():
            frecv[slot] = total

        @pl.when(is_self(u, s) == 0)
        def _():
            fsend_copy(q, 0, u, s).start()

        @pl.when((i != j) & (is_self(s, u) == 1))
        def _():
            frecv[slot] = total

        @pl.when((i != j) & (is_self(s, u) == 0))
        def _():
            fsend_copy(q, 1, s, u).start()

        return carry

    lax.fori_loop(0, 9, final_loop, 0)

    def collect(s, carry):
        straight_sum, mirror_sum = carry
        xs, zs = s // 4, lax.rem(s, 4)
        xh = xs // 2
        kr = lax.rem(xhi + 2 - xh, 2) * 4 + lax.rem(z + 4 - zs, 4)
        kc = lax.rem(b // 4 + 2 - xh, 2) * 4 + lax.rem(lax.rem(b, 4) + 4 - zs, 4)
        hi, lo = jnp.maximum(kr, kc), jnp.minimum(kr, kc)
        yt = lax.rem(hi * (hi + 1) // 2 + lo, 4)
        mine = jnp.where(s == slot, 1, 0) * jnp.where(yt == y, 1, 0)

        @pl.when(mine == 0)
        def _():
            pltpu.make_async_remote_copy(
                src_ref=fsend.at[0],
                dst_ref=frecv.at[s],
                send_sem=fs.at[0, 0],
                recv_sem=fr.at[s],
                device_id=dev(b, g, c),
                device_id_type=MESH,
            ).wait_recv()

        value = frecv[s]
        straight = jnp.where(kr >= kc, 1, 0).astype(F32)
        return straight_sum + value * straight, mirror_sum + value * (1.0 - straight)

    zero = jnp.zeros((64, 128), F32)
    straight_sum, mirror_sum = lax.fori_loop(0, 16, collect, (zero, zero))
    bpad[...] = jnp.zeros((128, 128), F32)
    bpad[pl.ds(pl.multiple_of(c * 64, 64), 64), :] = mirror_sum
    bt[...] = bpad[...].T
    swap = pltpu.make_async_remote_copy(
        src_ref=bt.at[pl.ds(pl.multiple_of(pc * 64, 64), 64)],
        dst_ref=drecv,
        send_sem=ds,
        recv_sem=dr,
        device_id=dev(b, g, pc),
        device_id_type=MESH,
    )
    swap.start()
    value = straight_sum + bt[pl.ds(pl.multiple_of(c * 64, 64), 64), :]
    swap.wait_recv()
    value = (value + drecv[...]) * scale
    row = lax.broadcasted_iota(jnp.int32, (64, 128), 0) + (g * 128 + c * 64)
    col = lax.broadcasted_iota(jnp.int32, (64, 128), 1) + b * 128
    out[...] = jnp.where(row == col, jnp.float32(0.0), value)

    swap.wait_send()
    for k in range(1, 8):
        p1(k).wait_send()
    for k in range(8):
        fwd(k).wait_send()

    def drain_y(t, carry):
        @pl.when(lax.rem(t, 4) != y)
        def _():
            ysend(t).wait_send()

        return carry

    lax.fori_loop(0, TILES, drain_y, 0)

    def drain_f(q, carry):
        i, j = pair_of(q * 4 + y)
        s, u = member(i), member(j)

        @pl.when(is_self(u, s) == 0)
        def _():
            fsend_copy(q, 0, u, s).wait_send()

        @pl.when((i != j) & (is_self(s, u) == 0))
        def _():
            fsend_copy(q, 1, s, u).wait_send()

        return carry

    lax.fori_loop(0, 9, drain_f, 0)


def body(coeffs):
    num_bands = coeffs.shape[3] // W * lax.axis_size("band")
    scale = W * K / num_bands
    dma = pltpu.SemaphoreType.DMA
    return pl.pallas_call(
        functools.partial(kernel, scale),
        name="coherence",
        out_shape=jax.ShapeDtypeStruct((64, 128), F32),
        in_specs=[pl.BlockSpec(memory_space=pl.ANY)],
        out_specs=pl.BlockSpec(memory_space=pltpu.VMEM),
        scratch_shapes=[
            pltpu.VMEM((8, 2, 8, 64, 128), BF16),
            pltpu.VMEM((8, 8, 64, 256), BF16),
            pltpu.VMEM((8, 2, 8, 64, 256), BF16),
            pltpu.VMEM((8, 128, 256), BF16),
            pltpu.VMEM((8, 8, 8, 128), F32),
            pltpu.VMEM((8, 64, 128), F32),
            pltpu.VMEM((TILES, 64, 128), F32),
            pltpu.VMEM((9, 3, 64, 128), F32),
            pltpu.VMEM((9, 64, 128), F32),
            pltpu.VMEM((16, 64, 128), F32),
            pltpu.VMEM((128, 128), F32),
            pltpu.VMEM((128, 128), F32),
            pltpu.VMEM((64, 128), F32),
            dma((8,)),
            dma((8,)),
            dma((8,)),
            dma((8,)),
            dma((8,)),
            dma((TILES,)),
            dma((9, 3)),
            dma((9, 2)),
            dma((16,)),
            dma,
            dma,
        ],
        compiler_params=pltpu.CompilerParams(
            collective_id=0, has_side_effects=True, vmem_limit_bytes=48 * 2**20
        ),
    )(coeffs)


def solution(mesh):
    return jax.shard_map(
        body,
        mesh=mesh,
        in_specs=(P(None, None, "chan", "band"),),
        out_specs=P("chan", "band"),
        check_vma=False,
    )
```

time: 329 us -> 67 us (0.20)
  the two profiles are of different devices: /device:TPU:9 before, /device:TPU:1 now
where the time goes in v1:
time: 67 us; the launch traced here: 66.9 us
  Pallas kernels  64.6 us (96%)
  local copies, waits for them, and re-layouts  2.21 us (3%)
    pallas_call x1, Pallas kernels, body(): pl.pallas_call(functools.partial(kernel, scale), name='coherence', out_sh...  64.6 us
    unnamed x3, local copies, waits for them, and re-layouts  2.21 us

profile of v1, /device:TPU:1, one launch (start us, length us, event | category | flops | bytes accessed | tf_op | source)
XLA Modules:
  0.0 66.9 jit_solution(11293977621184142973)
XLA Ops:
  0.0 0.0 copy-start
  0.0 1.6 %copy-done = bf16[2,8,64,1024]{3,2,1,0:T(8,128)(2,1)S(1)} copy-done((bf16[2,8,64,1024]{3,2,1,0:T(8,128)(2,1)S(1)}, bf16[2,8,64,1024]{3,2,1,0:T(8,128)(2,1)}, u32[]{:S(2)}) %copy-start) | copy-done | bytes 2097176
  1.6 64.6 %coherence.1 = f32[64,128]{1,0:T(8,128)S(1)} custom-call(bf16[2,8,64,1024]{3,2,1,0:T(8,128)(2,1)S(1)} %copy-done), custom_call_target="tpu_custom_call" | custom-call | tf_op jit(solution)/shard_map/coherence/pallas_call | solution.py:326
  66.2 0.6 copy.3
Async XLA Ops:
  0.0 1.6 %copy-start = (bf16[2,8,64,1024]{3,2,1,0:T(8,128)(2,1)S(1)}, bf16[2,8,64,1024]{3,2,1,0:T(8,128)(2,1)}, u32[]{:S(2)}) copy-start(bf16[2,8,64,1024]{3,2,1,0:T(8,128)(2,1)} %cx.1) | copy-start | bytes 6291460

commit v2 on v0

v2 whole, which is shorter than its diff:
```python
import functools

import jax
import jax.numpy as jnp
from jax import lax
from jax.experimental import pallas as pl
from jax.experimental.pallas import tpu as pltpu
from jax.sharding import PartitionSpec as P

K = 8
W = 16
EPS = 1e-06
MESH = pl.DeviceIdType.MESH
TILES = 36
F32 = jnp.float32
BF16 = jnp.bfloat16


def nt_dot(a, b):
    return lax.dot_general(a, b, (((1,), (1,)), ((), ())), preferred_element_type=F32)


def relayout(src, dst):
    group = lax.broadcasted_iota(jnp.int32, (16, 128), 1) // 16
    bits = [(group // (1 << s)) % 2 == 1 for s in range(3)]
    for part in range(2):
        for r in range(4):
            rows = pl.ds(r * 16, 16)
            vals = []
            for k in range(8):
                v = src[part, k, rows, :].astype(F32)
                vals.append(v if k == 0 else pltpu.roll(v, 16 * k, 1))
            for s in range(3):
                vals = [jnp.where(bits[s], vals[(m + (1 << s)) % 8], vals[m]) for m in range(8)]
            for w in range(8):
                dst[w, rows, part * 128 : (part + 1) * 128] = vals[(8 - w) % 8].astype(BF16)


def split_square(x):
    wide = x.astype(F32)
    square = wide * wide
    high = square.astype(BF16)
    low = (square - high.astype(F32)).astype(BF16)
    return high, low


RANK = (0, 4, 2, 7, 1, 6, 3, 5)
ISSUE = (4, 3, 2, 7, 6, 1, 5)
GROUPS = ((0, 4), (1, 7), (2, 6), (3, 5))
PHASES = ((0, 1, 2, 3, 4), (5,), (6,), (7,))


def lookup(table, index):
    value = 0
    for n, entry in enumerate(table):
        if entry:
            value = value + jnp.where(index == n, entry, 0)
    return value


def spans(first, last):
    out, j = [], first
    for size in (4, 2, 1):
        while j + size <= last:
            out.append((j, size))
            j += size
    return out


def slot_of(i, j):
    return i * (i + 1) // 2 + j


def group_tiles(group, steps):
    return [(i, j) for i in steps for j in GROUPS[group] if j <= i]


def kernel(
    scale, cx, out, xin, sbuf, rbuf, lhs, squares, prow, precv, rowi, coli, xt, tacc, yrecv, fsend, frecv,
    bpad, bt, drecv, in_s, p1s, p1r, fws, fwr, pps, ppr, ys, yr, fs, fr, ds, dr,
):
    b = lax.axis_index("band")
    ch = lax.axis_index("chan")
    y, xlo = b // 2, b % 2
    g, c = ch // 2, ch % 2
    xhi, z = g // 4, g % 4
    x = xhi * 2 + xlo
    pc = 1 - c

    flipped = (z, z + 1 - 2 * lax.rem(z, 2), lax.rem(z + 2, 4), 3 - z)

    def member(k):
        return lax.rem(xhi + k // 4, 2) * 4 + flipped[k % 4]

    def dev(band, grp, core):
        return (band, grp * 2 + core)

    barrier = pltpu.get_barrier_semaphore()
    for dx in range(4):
        for dz in range(4):
            if dx or dz:
                xo, zo = lax.rem(x + dx, 4), lax.rem(z + dz, 4)
                pl.semaphore_signal(
                    barrier,
                    inc=1,
                    device_id=dev(y * 2 + xo % 2, (xo // 2) * 4 + zo, c),
                    device_id_type=MESH,
                )
    pl.semaphore_signal(barrier, inc=1, device_id=dev(b, g, pc), device_id_type=MESH)
    for r in range(1, 4):
        pl.semaphore_signal(
            barrier, inc=1, device_id=dev(lax.rem(y + r, 4) * 2 + xlo, g, c), device_id_type=MESH
        )

    order = ISSUE + (0,)
    load_parts = ((0, 1), (1, 2), (3, 5))

    def load(n, part):
        at = pl.multiple_of(member(order[n]) * 128, 128)
        return pltpu.make_async_copy(cx.at[:, :, :, pl.ds(at, 128)], xin.at[n], in_s.at[part])

    for part, (first, count) in enumerate(load_parts):
        for n in range(first, first + count):
            load(n, part).start()

    def load_wait(part):
        first, count = load_parts[part]
        block = xin.at[pl.ds(first, count)]
        pltpu.make_async_copy(block, block, in_s.at[part]).wait()

    def p1(k):
        rank = RANK.index(k)
        return pltpu.make_async_remote_copy(
            src_ref=sbuf.at[k],
            dst_ref=rbuf.at[rank, c],
            send_sem=p1s,
            recv_sem=p1r.at[rank],
            device_id=dev(b, member(k), c),
            device_id_type=MESH,
        )

    def fwd(i):
        return pltpu.make_async_remote_copy(
            src_ref=rbuf.at[i, c],
            dst_ref=rbuf.at[i, c],
            send_sem=fws,
            recv_sem=fwr.at[i],
            device_id=dev(b, g, pc),
            device_id_type=MESH,
        )

    def pfwd(i):
        return pltpu.make_async_remote_copy(
            src_ref=prow.at[i],
            dst_ref=precv.at[i],
            send_sem=pps,
            recv_sem=ppr.at[i],
            device_id=dev(b, g, pc),
            device_id_type=MESH,
        )

    with jax.named_scope("relayout"):
        load_wait(0)
        relayout(xin.at[0], sbuf.at[ISSUE[0]])
        load_wait(1)
        for n in (1, 2):
            relayout(xin.at[n], sbuf.at[ISSUE[n]])
    with jax.named_scope("bar"):
        pl.semaphore_wait(barrier, 19)
    for k in ISSUE[:3]:
        p1(k).start()
    with jax.named_scope("relayout2"):
        load_wait(2)
        for n in range(3, 7):
            relayout(xin.at[n], sbuf.at[ISSUE[n]])
            p1(ISSUE[n]).start()
    relayout(xin.at[7], rbuf.at[0, c])
    fwd(0).start()

    ones_col = jnp.ones((128, 256), BF16)
    band_row = lax.broadcasted_iota(jnp.int32, (8, 128), 0)
    own_lane = (
        lax.broadcasted_iota(jnp.int32, (64, 128), 0) + c * 64
        == lax.broadcasted_iota(jnp.int32, (64, 128), 1)
    )

    chunks = [member(k) for k in RANK]

    planes = [chunks[group[0]] // 2 for group in GROUPS]
    group_of = {j: n for n, group in enumerate(GROUPS) for j in group}
    phase_of = {i: n for n, steps in enumerate(PHASES) for i in steps}
    slot = x * 4 + z

    def bulk(count, send_sem, recv_sem):
        block = tacc.at[pl.ds(0, count)]
        return pltpu.make_async_remote_copy(
            src_ref=block,
            dst_ref=block,
            send_sem=send_sem,
            recv_sem=recv_sem,
            device_id=dev(b, g, pc),
            device_id_type=MESH,
        )

    def ysend(i, j):
        group = group_of[j]
        at = lax.rem(y + 7 - planes[group], 4)
        return pltpu.make_async_remote_copy(
            src_ref=tacc.at[slot_of(i, j)],
            dst_ref=yrecv.at[slot_of(i, j), at],
            send_sem=ys.at[i // 7, group],
            recv_sem=yr.at[phase_of[i], at],
            device_id=dev(planes[group] * 2 + xlo, g, c),
            device_id_type=MESH,
        )

    def ysent(late, steps):
        for group in range(4):

            @pl.when(y != planes[group])
            def _():
                bulk(len(group_tiles(group, steps)), ys.at[late, group], fr).wait_send()

    def tiles(i, first, count):
        width = 128 * min(count, 2)
        for j in range(first, first + count, 2):
            acc = jnp.zeros((64, width), F32)
            for w in range(8):
                if j == 7:
                    prod = nt_dot(lhs[w], rbuf[j, :, w].reshape(width, 256))
                else:
                    prod = jnp.dot(
                        lhs[w],
                        xt[w, :, j * 128 : j * 128 + width],
                        preferred_element_type=F32,
                    )
                re, im = prod[:64], prod[64:]
                col = coli[w]
                if width == 256:
                    col = jnp.concatenate((col, col), axis=1)
                acc = acc + (re * re + im * im) * (
                    col * rowi[w : w + 1, j * 128 : j * 128 + width]
                )
            for n in range(width // 128):
                tacc[slot_of(i, j + n)] = acc[:, n * 128 : (n + 1) * 128]
        for j in range(first, first + count):

            @pl.when(y != planes[group_of[j]])
            def _():
                ysend(i, j).start()

    def fsend_copy(i, j, side):
        row, col = (chunks[i], chunks[j]) if side == 0 else (chunks[j], chunks[i])
        return pltpu.make_async_remote_copy(
            src_ref=fsend.at[slot_of(i, j)],
            dst_ref=frecv.at[slot],
            send_sem=fs,
            recv_sem=fr,
            device_id=dev(col, row, c),
            device_id_type=MESH,
        )

    def is_own(i, j):
        return (b == chunks[j]) & (g == chunks[i])

    def mirror(i, j):
        if i == j:
            return
        if j != 0:
            fsend_copy(i, j, 1).start()
            return

        @pl.when(jnp.logical_not(is_own(j, i)))
        def _():
            fsend_copy(i, j, 1).start()

    def final(phase, mirrored):
        for group in range(4):

            @pl.when(y == planes[group])
            def _():
                members = group_tiles(group, PHASES[phase])
                with jax.named_scope(f"wait_y{phase}"):
                    for r in range(3):
                        bulk(len(members), fs, yr.at[phase, r]).wait_recv()
                for i, j in members:
                    t = slot_of(i, j)
                    total = tacc[t]
                    for r in range(3):
                        total = total + yrecv[t, r]
                    fsend[t] = total
                    if j != 0:
                        fsend_copy(i, j, 0).start()
                    elif i != 0:
                        fsend_copy(i, j, 0).start()

                        @pl.when(is_own(j, i))
                        def _():
                            frecv[slot] = total
                    else:

                        @pl.when(is_own(i, j))
                        def _():
                            frecv[slot] = total

                        @pl.when(jnp.logical_not(is_own(i, j)))
                        def _():
                            fsend_copy(i, j, 0).start()

                    if mirrored:
                        mirror(i, j)

    for i in range(8):
        if i > 0:
            with jax.named_scope(f"wait_p1_{i}"):
                p1(RANK[i]).wait_recv()
            fwd(i).start()
        if i == 7:
            with jax.named_scope("final_a"):
                final(0, False)
        with jax.named_scope("power"):
            for w in range(8):
                v = rbuf[i, c, w]
                lhs[w, 0:64, :] = v
                lhs[w, 64:128, 0:128] = v[:, 128:]
                lhs[w, 64:128, 128:256] = -v[:, :128]
                squares[0, w], squares[1, w] = split_square(v)
            sums = nt_dot(squares[...].reshape(1024, 256), ones_col)
            sums = sums[:512] + sums[512:] + EPS
            coli[...] = (1.0 / sums).reshape(8, 64, 128)
            row = jnp.zeros((8, 128), F32)
            for w in range(8):
                own = jnp.where(own_lane, sums[w * 64 : (w + 1) * 64], 0.0)
                own = jnp.sum(own, axis=0, keepdims=True)
                row = jnp.where(band_row == w, own, row)
            prow[i] = row
            pfwd(i).start()
        before = i if i == 7 else i // 2 * 2
        with jax.named_scope("tiles"):
            for first, count in spans(0, before):
                tiles(i, first, count)
        with jax.named_scope("wait_fwd"):
            fwd(i).wait_recv()
            pfwd(i).wait_recv()
        with jax.named_scope("tiles_last"):
            rowi[:, i * 128 : (i + 1) * 128] = 1.0 / (prow[i] + precv[i])
            if i < 7:
                for w in range(8):
                    both = rbuf[i, :, w].reshape(128, 256)
                    xt[w, :, i * 128 : (i + 1) * 128] = both.T
            tiles(i, before, i + 1 - before)

    with jax.named_scope("final_b"):
        final(1, False)
        final(2, False)
    with jax.named_scope("sent_y7"):
        ysent(1, (7,))
    with jax.named_scope("mirror"):
        for group in range(4):

            @pl.when(y == planes[group])
            def _():
                for i, j in group_tiles(group, range(7)):
                    mirror(i, j)

    with jax.named_scope("final_c"):
        final(3, True)

    flags = []
    for s in range(16):
        xs, zs = s // 4, s % 4
        xh = xs // 2
        differ = tuple(zs ^ n for n in range(4))
        kr = lax.rem(g // 4 + xh, 2) * 4 + lookup(differ, lax.rem(g, 4))
        kc = lax.rem(b // 4 + xh, 2) * 4 + lookup(differ, lax.rem(b, 4))
        ranks = tuple(RANK.index(n) for n in range(8))
        kr, kc = lookup(ranks, kr), lookup(ranks, kc)
        flags.append(jnp.where(kr >= kc, 1, 0).astype(F32))

    with jax.named_scope("drain"):
        block = sbuf.at[pl.ds(1, 7)]
        pltpu.make_async_remote_copy(
            src_ref=block,
            dst_ref=block,
            send_sem=p1s,
            recv_sem=p1r.at[0],
            device_id=dev(b, g, pc),
            device_id_type=MESH,
        ).wait_send()
        pltpu.make_async_remote_copy(
            src_ref=sbuf,
            dst_ref=sbuf,
            send_sem=fws,
            recv_sem=p1r.at[0],
            device_id=dev(b, g, pc),
            device_id_type=MESH,
        ).wait_send()
        pltpu.make_async_remote_copy(
            src_ref=prow,
            dst_ref=precv,
            send_sem=pps,
            recv_sem=p1r.at[0],
            device_id=dev(b, g, pc),
            device_id_type=MESH,
        ).wait_send()
        ysent(0, range(7))

    with jax.named_scope("collect"):

        @pl.when(y == planes[0])
        def _():
            bulk(15, fs, fr).wait_recv()

        @pl.when(y != planes[0])
        def _():
            bulk(16, fs, fr).wait_recv()

    straight_sum = jnp.zeros((64, 128), F32)
    mirror_sum = jnp.zeros((64, 128), F32)
    for s, weight in enumerate(flags):
        value = frecv[s]
        straight_sum = straight_sum + value * weight
        mirror_sum = mirror_sum + value * (1.0 - weight)

    bpad[...] = jnp.zeros((128, 128), F32)
    bpad[pl.ds(pl.multiple_of(c * 64, 64), 64), :] = mirror_sum
    bt[...] = bpad[...].T
    swap = pltpu.make_async_remote_copy(
        src_ref=bt.at[pl.ds(pl.multiple_of(pc * 64, 64), 64)],
        dst_ref=drecv,
        send_sem=ds,
        recv_sem=dr,
        device_id=dev(b, g, pc),
        device_id_type=MESH,
    )
    swap.start()
    value = straight_sum + bt[pl.ds(pl.multiple_of(c * 64, 64), 64), :]
    with jax.named_scope("drain_f"):
        for group in range(4):

            @pl.when(y == planes[group])
            def _():
                count = 2 * len(group_tiles(group, range(8))) - 2 - (1 if group == 0 else 0)
                bulk(count, fs, fr).wait_send()

    with jax.named_scope("swap"):
        swap.wait_recv()
    value = (value + drecv[...]) * scale
    row = lax.broadcasted_iota(jnp.int32, (64, 128), 0) + (g * 128 + c * 64)
    col = lax.broadcasted_iota(jnp.int32, (64, 128), 1) + b * 128
    out[...] = jnp.where(row == col, jnp.float32(0.0), value)
    swap.wait_send()


def body(coeffs):
    num_bands = coeffs.shape[3] // W * lax.axis_size("band")
    scale = W * K / num_bands
    dma = pltpu.SemaphoreType.DMA
    return pl.pallas_call(
        functools.partial(kernel, scale),
        name="coherence",
        out_shape=pltpu.VMEM((64, 128), F32),
        in_specs=[pl.BlockSpec(memory_space=pl.ANY)],
        out_specs=pl.BlockSpec(memory_space=pltpu.VMEM),
        scratch_shapes=[
            pltpu.VMEM((8, 2, 8, 64, 128), BF16),
            pltpu.VMEM((8, 8, 64, 256), BF16),
            pltpu.VMEM((8, 2, 8, 64, 256), BF16),
            pltpu.VMEM((8, 128, 256), BF16),
            pltpu.VMEM((2, 8, 64, 256), BF16),
            pltpu.VMEM((8, 8, 128), F32),
            pltpu.VMEM((8, 8, 128), F32),
            pltpu.VMEM((8, 1024), F32),
            pltpu.VMEM((8, 64, 128), F32),
            pltpu.VMEM((8, 256, 1024), BF16),
            pltpu.VMEM((TILES, 64, 128), F32),
            pltpu.VMEM((TILES, 3, 64, 128), F32),
            pltpu.VMEM((TILES, 64, 128), F32),
            pltpu.VMEM((16, 64, 128), F32),
            pltpu.VMEM((128, 128), F32),
            pltpu.VMEM((128, 128), F32),
            pltpu.VMEM((64, 128), F32),
            dma((3,)),
            dma,
            dma((8,)),
            dma,
            dma((8,)),
            dma,
            dma((8,)),
            dma((2, 4)),
            dma((4, 3)),
            dma,
            dma,
            dma,
            dma,
        ],
        compiler_params=pltpu.CompilerParams(
            collective_id=0, has_side_effects=True, vmem_limit_bytes=63 * 2**20
        ),
    )(coeffs)


def solution(mesh):
    return jax.shard_map(
        body,
        mesh=mesh,
        in_specs=(P(None, None, "chan", "band"),),
        out_specs=P("chan", "band"),
        check_vma=False,
    )
```

time: 329 us -> 54.1 us (0.16); the launches traced: 325 us -> 54 us
  waiting for transfers between devices: 181 us -> 0 us
  local copies, waits for them, and re-layouts: 58.1 us -> 0.62 us
  Pallas kernels: 0 us -> 53.4 us
  other arithmetic: 38.6 us -> 0 us
  matrix products: 25.2 us -> 0 us
  between operations: 13.5 us -> 0.01 us
  blocking collectives: 8.74 us -> 0 us
    all_gather x1 -> x0, waiting for transfers between devices: 181 us -> none  [body(): piece = lax.all_gather(coeffs, 'chan', axis=2, tiled=True)]
    pallas_call x0 -> x1, Pallas kernels: none -> 53.4 us  [body(): pl.pallas_call(functools.partial(kernel, scale), name='coherence', out_sh...]
    all_gather x1 -> x0, local copies, waits for them, and re-layouts: 45.1 us -> none  [body(): piece = lax.all_gather(coeffs, 'chan', axis=2, tiled=True)]
    reduce_sum x6 -> x0, other arithmetic: 33.8 us -> none  [the longest x2 21.4 us: body(): piece_power = jnp.sum(wide_piece * wide_piece, axis=(0, 1, 4)).T + epsilon]
    dot_general x1 -> x0, matrix products: 25.2 us -> none  [body(): jnp.einsum('pkinw,pkjnw->nij', left_side, right_side, preferred_element_t...]
    all_to_all x1 -> x0, blocking collectives: 8.74 us -> none  [sent_and_summed(): lax.all_to_all(in_blocks(shard, dim, length), axis, 0, 0, tiled=True)]
    unnamed x5 -> x1, local copies, waits for them, and re-layouts: 7.43 us -> 0.62 us
    reduce_sum x2 -> x0, local copies, waits for them, and re-layouts: 5.54 us -> none  [the longest x1 5.34 us: body(): piece_power = jnp.sum(wide_piece * wide_piece, axis=(0, 1, 4)).T + epsilon]
  transfers between devices with their start and end apart: 1 -> 0, of which waited for: 1 -> 0; matrix products, arithmetic and copies ran while one was open for 2% -> 0% of each run, Pallas kernels for 0% -> 0%
where the time goes in v2:
time: 54.1 us; the launch traced here: 54 us
  Pallas kernels  53.4 us (99%)
  local copies, waits for them, and re-layouts  0.62 us (1%)
    pallas_call x1, Pallas kernels, body(): pl.pallas_call(functools.partial(kernel, scale), name='coherence', out_sh...  53.4 us

profile of v2, /device:TPU:9, one launch (start us, length us, event | category | flops | bytes accessed | tf_op | source)
XLA Modules:
  0.0 54.0 jit_solution(2464977526069860517)
XLA Ops:
  0.0 53.4 %coherence.1 = f32[64,128]{1,0:T(8,128)S(1)} custom-call(bf16[2,8,64,1024]{3,2,1,0:T(8,128)(2,1)} %cx.1), custom_call_target="tpu_custom_call" | custom-call | tf_op jit(solution)/shard_map/coherence/pallas_call | solution.py:459
  53.4 0.6 %copy.3 = f32[64,128]{1,0:T(8,128)} copy(f32[64,128]{1,0:T(8,128)S(1)} %coherence.1) | data formatting | bytes 65536

commit v3 on v2

--- a/solution.py
+++ b/solution.py
@@ -36,18 +36,9 @@
                 dst[w, rows, part * 128 : (part + 1) * 128] = vals[(8 - w) % 8].astype(BF16)
 
 
-def split_square(x):
-    wide = x.astype(F32)
-    square = wide * wide
-    high = square.astype(BF16)
-    low = (square - high.astype(F32)).astype(BF16)
-    return high, low
-
-
-RANK = (0, 4, 2, 7, 1, 6, 3, 5)
-ISSUE = (4, 3, 2, 7, 6, 1, 5)
+RANK = (0, 4, 2, 6, 1, 7, 3, 5)
+ISSUE = (4, 2, 3, 6, 7, 1, 5)
 GROUPS = ((0, 4), (1, 7), (2, 6), (3, 5))
-PHASES = ((0, 1, 2, 3, 4), (5,), (6,), (7,))
 
 
 def lookup(table, index):
@@ -71,13 +62,9 @@
     return i * (i + 1) // 2 + j
 
 
-def group_tiles(group, steps):
-    return [(i, j) for i in steps for j in GROUPS[group] if j <= i]
-
-
 def kernel(
-    scale, cx, out, xin, sbuf, rbuf, lhs, squares, prow, precv, rowi, coli, xt, tacc, yrecv, fsend, frecv,
-    bpad, bt, drecv, in_s, p1s, p1r, fws, fwr, pps, ppr, ys, yr, fs, fr, ds, dr,
+    scale, cx, out, xin, sbuf, rbuf, lhs, prow, precv, rowi, coli, xt, tacc, yrecv, fsend, frecv,
+    bpad, bt, whole, drecv, in_s, p1s, p1r, fws, fwr, pps, ppr, ys, yr, fs, fr, ds, dr,
 ):
     b = lax.axis_index("band")
     ch = lax.axis_index("chan")
@@ -177,7 +164,6 @@
     relayout(xin.at[7], rbuf.at[0, c])
     fwd(0).start()
 
-    ones_col = jnp.ones((128, 256), BF16)
     band_row = lax.broadcasted_iota(jnp.int32, (8, 128), 0)
     own_lane = (
         lax.broadcasted_iota(jnp.int32, (64, 128), 0) + c * 64
@@ -186,9 +172,12 @@
 
     chunks = [member(k) for k in RANK]
 
-    planes = [chunks[group[0]] // 2 for group in GROUPS]
     group_of = {j: n for n, group in enumerate(GROUPS) for j in group}
-    phase_of = {i: n for n, steps in enumerate(PHASES) for i in steps}
+    heights = [value // 2 for value in chunks]
+
+    def plane(i, group):
+        return lax.rem(heights[i] + heights[GROUPS[group][0]], 4)
+
     slot = x * 4 + z
 
     def bulk(count, send_sem, recv_sem):
@@ -203,23 +192,16 @@
         )
 
     def ysend(i, j):
-        group = group_of[j]
-        at = lax.rem(y + 7 - planes[group], 4)
+        at_y = plane(i, group_of[j])
+        at = lax.rem(y + 7 - at_y, 4)
         return pltpu.make_async_remote_copy(
             src_ref=tacc.at[slot_of(i, j)],
             dst_ref=yrecv.at[slot_of(i, j), at],
-            send_sem=ys.at[i // 7, group],
-            recv_sem=yr.at[phase_of[i], at],
-            device_id=dev(planes[group] * 2 + xlo, g, c),
-            device_id_type=MESH,
-        )
-
-    def ysent(late, steps):
-        for group in range(4):
-
-            @pl.when(y != planes[group])
-            def _():
-                bulk(len(group_tiles(group, steps)), ys.at[late, group], fr).wait_send()
+            send_sem=ys.at[i // 7],
+            recv_sem=yr.at[i, at],
+            device_id=dev(at_y * 2 + xlo, g, c),
+            device_id_type=MESH,
+        )
 
     def tiles(i, first, count):
         width = 128 * min(count, 2)
@@ -245,7 +227,7 @@
                 tacc[slot_of(i, j + n)] = acc[:, n * 128 : (n + 1) * 128]
         for j in range(first, first + count):
 
-            @pl.when(y != planes[group_of[j]])
+            @pl.when(y != plane(i, group_of[j]))
             def _():
                 ysend(i, j).start()
 
@@ -256,81 +238,64 @@
             dst_ref=frecv.at[slot],
             send_sem=fs,
             recv_sem=fr,
-            device_id=dev(col, row, c),
-            device_id_type=MESH,
-        )
-
-    def is_own(i, j):
-        return (b == chunks[j]) & (g == chunks[i])
-
-    def mirror(i, j):
-        if i == j:
+            device_id=dev(y * 2 + col % 2, row, c),
+            device_id_type=MESH,
+        )
+
+    def send_owner(i, j, side, total):
+        row, col = (i, j) if side == 0 else (j, i)
+        if row:
+            fsend_copy(i, j, side).start()
             return
-        if j != 0:
-            fsend_copy(i, j, 1).start()
-            return
-
-        @pl.when(jnp.logical_not(is_own(j, i)))
-        def _():
-            fsend_copy(i, j, 1).start()
-
-    def final(phase, mirrored):
+
+        @pl.when(chunks[col] % 2 == xlo)
+        def _():
+            frecv[slot] = total
+
+        @pl.when(chunks[col] % 2 != xlo)
+        def _():
+            fsend_copy(i, j, side).start()
+
+    def final(i):
         for group in range(4):
-
-            @pl.when(y == planes[group])
-            def _():
-                members = group_tiles(group, PHASES[phase])
-                with jax.named_scope(f"wait_y{phase}"):
-                    for r in range(3):
-                        bulk(len(members), fs, yr.at[phase, r]).wait_recv()
-                for i, j in members:
-                    t = slot_of(i, j)
-                    total = tacc[t]
-                    for r in range(3):
-                        total = total + yrecv[t, r]
-                    fsend[t] = total
-                    if j != 0:
-                        fsend_copy(i, j, 0).start()
-                    elif i != 0:
-                        fsend_copy(i, j, 0).start()
-
-                        @pl.when(is_own(j, i))
-                        def _():
-                            frecv[slot] = total
-                    else:
-
-                        @pl.when(is_own(i, j))
-                        def _():
-                            frecv[slot] = total
-
-                        @pl.when(jnp.logical_not(is_own(i, j)))
-                        def _():
-                            fsend_copy(i, j, 0).start()
-
-                    if mirrored:
-                        mirror(i, j)
+            members = [(i, j) for j in GROUPS[group] if j <= i]
+            if members:
+
+                @pl.when(y == plane(i, group))
+                def _():
+                    with jax.named_scope(f"wait_y{i}"):
+                        for r in range(3):
+                            bulk(len(members), fs, yr.at[i, r]).wait_recv()
+                    for i_, j in members:
+                        t = slot_of(i, j)
+                        total = tacc[t]
+                        for r in range(3):
+                            total = total + yrecv[t, r]
+                        fsend[t] = total
+                        send_owner(i, j, 0, total)
+                        if i != j:
+                            send_owner(i, j, 1, total)
 
     for i in range(8):
         if i > 0:
             with jax.named_scope(f"wait_p1_{i}"):
                 p1(RANK[i]).wait_recv()
             fwd(i).start()
-        if i == 7:
-            with jax.named_scope("final_a"):
-                final(0, False)
         with jax.named_scope("power"):
+            sums = []
             for w in range(8):
                 v = rbuf[i, c, w]
                 lhs[w, 0:64, :] = v
                 lhs[w, 64:128, 0:128] = v[:, 128:]
                 lhs[w, 64:128, 128:256] = -v[:, :128]
-                squares[0, w], squares[1, w] = split_square(v)
-            sums = nt_dot(squares[...].reshape(1024, 256), ones_col)
-            sums = sums[:512] + sums[512:] + EPS
-            coli[...] = (1.0 / sums).reshape(8, 64, 128)
+                wide = v.astype(F32)
+                wide = wide * wide
+                total = jnp.sum(wide[:, :128] + wide[:, 128:], axis=1, keepdims=True) + EPS
+                sums.append(jnp.broadcast_to(total, (64, 128)))
+                coli[w] = jnp.broadcast_to(1.0 / total, (64, 128))
             row = jnp.zeros((8, 128), F32)
             for w in range(8):
-                own = jnp.where(own_lane, sums[w * 64 : (w + 1) * 64], 0.0)
+                own = jnp.where(own_lane, sums[w], 0.0)
                 own = jnp.sum(own, axis=0, keepdims=True)
                 row = jnp.where(band_row == w, own, row)
             prow[i] = row
@@ -339,6 +304,10 @@
         with jax.named_scope("tiles"):
             for first, count in spans(0, before):
                 tiles(i, first, count)
+        if i == 7:
+            with jax.named_scope("final_a"):
+                for m in range(6):
+                    final(m)
         with jax.named_scope("wait_fwd"):
             fwd(i).wait_recv()
             pfwd(i).wait_recv()
@@ -351,28 +320,18 @@
             tiles(i, before, i + 1 - before)
 
     with jax.named_scope("final_b"):
-        final(1, False)
-        final(2, False)
-    with jax.named_scope("sent_y7"):
-        ysent(1, (7,))
-    with jax.named_scope("mirror"):
-        for group in range(4):
-
-            @pl.when(y == planes[group])
-            def _():
-                for i, j in group_tiles(group, range(7)):
-                    mirror(i, j)
-
+        final(6)
     with jax.named_scope("final_c"):
-        final(3, True)
-
+        final(7)
+
+    col_chunk = lax.rem(y + 4 - g // 2, 4) * 2 + xlo
     flags = []
     for s in range(16):
         xs, zs = s // 4, s % 4
         xh = xs // 2
         differ = tuple(zs ^ n for n in range(4))
         kr = lax.rem(g // 4 + xh, 2) * 4 + lookup(differ, lax.rem(g, 4))
-        kc = lax.rem(b // 4 + xh, 2) * 4 + lookup(differ, lax.rem(b, 4))
+        kc = lax.rem(col_chunk // 4 + xh, 2) * 4 + lookup(differ, lax.rem(col_chunk, 4))
         ranks = tuple(RANK.index(n) for n in range(8))
         kr, kc = lookup(ranks, kr), lookup(ranks, kc)
         flags.append(jnp.where(kr >= kc, 1, 0).astype(F32))
@@ -403,17 +362,18 @@
             device_id=dev(b, g, pc),
             device_id_type=MESH,
         ).wait_send()
-        ysent(0, range(7))
+        bulk(6, ys.at[1], fr).wait_send()
+
+        @pl.when(lax.rem(y, 2) == 0)
+        def _():
+            bulk(20, ys.at[0], fr).wait_send()
+
+        @pl.when(lax.rem(y, 2) == 1)
+        def _():
+            bulk(22, ys.at[0], fr).wait_send()
 
     with jax.named_scope("collect"):
-
-        @pl.when(y == planes[0])
-        def _():
-            bulk(15, fs, fr).wait_recv()
-
-        @pl.when(y != planes[0])
-        def _():
-            bulk(16, fs, fr).wait_recv()
+        bulk(15, fs, fr).wait_recv()
 
     straight_sum = jnp.zeros((64, 128), F32)
     mirror_sum = jnp.zeros((64, 128), F32)
@@ -425,31 +385,46 @@
     bpad[...] = jnp.zeros((128, 128), F32)
     bpad[pl.ds(pl.multiple_of(c * 64, 64), 64), :] = mirror_sum
     bt[...] = bpad[...].T
-    swap = pltpu.make_async_remote_copy(
-        src_ref=bt.at[pl.ds(pl.multiple_of(pc * 64, 64), 64)],
-        dst_ref=drecv,
-        send_sem=ds,
-        recv_sem=dr,
-        device_id=dev(b, g, pc),
-        device_id_type=MESH,
-    )
-    swap.start()
-    value = straight_sum + bt[pl.ds(pl.multiple_of(c * 64, 64), 64), :]
+    whole[...] = straight_sum + bt[pl.ds(pl.multiple_of(c * 64, 64), 64), :]
+
+    def deliver(part):
+        src = whole if part == 0 else bt.at[pl.ds(pl.multiple_of(pc * 64, 64), 64)]
+        return pltpu.make_async_remote_copy(
+            src_ref=src,
+            dst_ref=drecv.at[part],
+            send_sem=ds,
+            recv_sem=dr,
+            device_id=dev(col_chunk, g, c if part == 0 else pc),
+            device_id_type=MESH,
+        )
+
+    deliver(1).start()
+
+    @pl.when(col_chunk == b)
+    def _():
+        drecv[0] = whole[...]
+
+    @pl.when(col_chunk != b)
+    def _():
+        deliver(0).start()
+
     with jax.named_scope("drain_f"):
-        for group in range(4):
-
-            @pl.when(y == planes[group])
-            def _():
-                count = 2 * len(group_tiles(group, range(8))) - 2 - (1 if group == 0 else 0)
-                bulk(count, fs, fr).wait_send()
+        bulk(15, fs, fr).wait_send()
 
     with jax.named_scope("swap"):
-        swap.wait_recv()
-    value = (value + drecv[...]) * scale
+
+        @pl.when(col_chunk == b)
+        def _():
+            bulk(1, ds, dr).wait()
+
+        @pl.when(col_chunk != b)
+        def _():
+            bulk(2, ds, dr).wait()
+
+    value = (drecv[0] + drecv[1]) * scale
     row = lax.broadcasted_iota(jnp.int32, (64, 128), 0) + (g * 128 + c * 64)
     col = lax.broadcasted_iota(jnp.int32, (64, 128), 1) + b * 128
     out[...] = jnp.where(row == col, jnp.float32(0.0), value)
-    swap.wait_send()
 
 
 def body(coeffs):
@@ -467,7 +442,6 @@
             pltpu.VMEM((8, 8, 64, 256), BF16),
             pltpu.VMEM((8, 2, 8, 64, 256), BF16),
             pltpu.VMEM((8, 128, 256), BF16),
-            pltpu.VMEM((2, 8, 64, 256), BF16),
             pltpu.VMEM((8, 8, 128), F32),
             pltpu.VMEM((8, 8, 128), F32),
             pltpu.VMEM((8, 1024), F32),
@@ -480,6 +454,7 @@
             pltpu.VMEM((128, 128), F32),
             pltpu.VMEM((128, 128), F32),
             pltpu.VMEM((64, 128), F32),
+            pltpu.VMEM((2, 64, 128), F32),
             dma((3,)),
             dma,
             dma((8,)),
@@ -487,8 +462,8 @@
             dma((8,)),
             dma,
             dma((8,)),
-            dma((2, 4)),
-            dma((4, 3)),
+            dma((2,)),
+            dma((8, 3)),
             dma,
             dma,
             dma,

time: 54.1 us -> 49.8 us (0.921); the launches traced: 54 us -> 49.1 us
  Pallas kernels: 53.4 us -> 48.4 us
    pallas_call x1, Pallas kernels: 53.4 us -> 48.4 us  [body(): pl.pallas_call(functools.partial(kernel, scale), name='coherence', out_sh...]
where the time goes in v3:
time: 49.8 us; the launch traced here: 49.1 us
  Pallas kernels  48.4 us (97%)
  local copies, waits for them, and re-layouts  0.62 us (1%)
    pallas_call x1, Pallas kernels, body(): pl.pallas_call(functools.partial(kernel, scale), name='coherence', out_sh...  48.4 us

profile of v3, /device:TPU:9, one launch (start us, length us, event | category | flops | bytes accessed | tf_op | source)
XLA Modules:
  0.0 49.1 jit_solution(10912908779442329107)
XLA Ops:
  0.0 48.4 %coherence.1 = f32[64,128]{1,0:T(8,128)S(1)} custom-call(bf16[2,8,64,1024]{3,2,1,0:T(8,128)(2,1)} %cx.1), custom_call_target="tpu_custom_call" | custom-call | tf_op jit(solution)/shard_map/coherence/pallas_call | solution.py:434
  48.5 0.6 %copy.3 = f32[64,128]{1,0:T(8,128)} copy(f32[64,128]{1,0:T(8,128)S(1)} %coherence.1) | data formatting | bytes 65536

commit v4 on v3

--- a/solution.py
+++ b/solution.py
@@ -152,15 +152,13 @@
         load_wait(1)
         for n in (1, 2):
             relayout(xin.at[n], sbuf.at[ISSUE[n]])
-    with jax.named_scope("bar"):
-        pl.semaphore_wait(barrier, 19)
-    for k in ISSUE[:3]:
-        p1(k).start()
-    with jax.named_scope("relayout2"):
         load_wait(2)
         for n in range(3, 7):
             relayout(xin.at[n], sbuf.at[ISSUE[n]])
-            p1(ISSUE[n]).start()
+    with jax.named_scope("bar"):
+        pl.semaphore_wait(barrier, 19)
+    for k in ISSUE:
+        p1(k).start()
     relayout(xin.at[7], rbuf.at[0, c])
     fwd(0).start()
 
@@ -306,7 +304,7 @@
                 tiles(i, first, count)
         if i == 7:
             with jax.named_scope("final_a"):
-                for m in range(6):
+                for m in range(5):
                     final(m)
         with jax.named_scope("wait_fwd"):
             fwd(i).wait_recv()
@@ -320,6 +318,7 @@
             tiles(i, before, i + 1 - before)
 
     with jax.named_scope("final_b"):
+        final(5)
         final(6)
     with jax.named_scope("final_c"):
         final(7)

time: 49.8 us -> 49.8 us (level)
  no operation moved by 1% of the time
where the time goes in v4:
time: 49.8 us; the launch traced here: 49.1 us
  Pallas kernels  48.4 us (97%)
  local copies, waits for them, and re-layouts  0.62 us (1%)
    pallas_call x1, Pallas kernels, body(): pl.pallas_call(functools.partial(kernel, scale), name='coherence', out_sh...  48.4 us

profile of v4, /device:TPU:9, one launch (start us, length us, event | category | flops | bytes accessed | tf_op | source)
XLA Modules:
  0.0 49.1 jit_solution(13343049825649777673)
XLA Ops:
  0.0 48.4 %coherence.1 = f32[64,128]{1,0:T(8,128)S(1)} custom-call(bf16[2,8,64,1024]{3,2,1,0:T(8,128)(2,1)} %cx.1), custom_call_target="tpu_custom_call" | custom-call | tf_op jit(solution)/shard_map/coherence/pallas_call | solution.py:433
  48.4 0.6 %copy.3 = f32[64,128]{1,0:T(8,128)} copy(f32[64,128]{1,0:T(8,128)S(1)} %coherence.1) | data formatting | bytes 65536
